TPU v7x, 32 devices: a whole 2x2x4 slice. The times are simulated.
32 devices in a mesh: row: 8 (over z, core), col: 4 (over y, x).
Axes of the slice: x: 2, y: 2, z: 4, core: 2. Of those that a mesh axis runs over, the one named last changes fastest.
Arguments:
- right_sides: float32 [4, 1024, 4096], P(None, 'row', 'col'), may hold values from -6 to 6
- low_left: bfloat16 [6, 4096, 128], P(None, 'col'), may hold values from -0.25 to 0.25
- low_right: bfloat16 [6, 4096, 128], P(None, 'col'), may hold values from -0.09375 to 0.09375
- up_left: bfloat16 [6, 4096, 128], P(None, 'col'), may hold values from -0.25 to 0.25
- up_right: bfloat16 [6, 4096, 128], P(None, 'col'), may hold values from -0.09375 to 0.09375
- low_ranks: int32 [6], replicated, may hold values from 1 to 4
- up_ranks: int32 [6], replicated, may hold values from 1 to 4
- inv_lower: bfloat16 [4, 4096, 4096], P(None, 'col', 'row'), may hold values from -0.09375 to 0.09375
- inv_upper: bfloat16 [4, 4096, 4096], P(None, 'col', 'row'), may hold values from -0.09375 to 0.09375
Outputs:
- solution: float32 [4, 1024, 4096], P(None, 'row', 'col')
Inputs may be any that keep to these rules, and one draw needn't show every extreme that they name: `low_ranks`: factor columns beyond 32 times this value are padding with arbitrary values and must be masked out. `up_ranks`: factor columns beyond 32 times this value are padding with arbitrary values and must be masked out.
All inputs are finite; a program needn't handle non-finite values.
Results may differ from a plain program's by a relative error of at most 0.03.
Values may be sent and summed in bfloat16 or wider, within the bound.
A program may use at most 64 MiB of HBM per device.

v0:
```python
import jax
import jax.numpy as jnp
import numpy as np
from jax import lax
from jax.sharding import PartitionSpec as P

RBLK = 32


def rank_mask(ranks, pair_index, rank_cols):
    columns = jnp.arange(rank_cols, dtype=jnp.int32)
    return (columns[None, :] < RBLK * ranks[pair_index][:, None]).astype(jnp.float32)


def times_inverse(block, inverse):
    return lax.dot_general(
        block, inverse, (((1,), (1,)), ((), ())), preferred_element_type=jnp.float32
    )


def sum_terms(moved, inverse):
    return times_inverse(moved, inverse)


def shards(
    right_sides, low_left, low_right, up_left, up_right, low_ranks, up_ranks, inv_lower, inv_upper
):
    tile_count = right_sides.shape[0]
    rank_cols = low_left.shape[2]
    residual = right_sides
    forward = []
    for section in range(tile_count):
        rounded = residual[section].astype(jnp.bfloat16)
        whole = lax.all_gather(rounded, "col", axis=1, tiled=True)
        moved = lax.all_to_all(whole, "row", split_axis=1, concat_axis=0, tiled=True)
        solved = lax.psum_scatter(
            sum_terms(moved, inv_lower[section]).astype(jnp.bfloat16),
            "row",
            scatter_dimension=0,
            tiled=True,
        ).astype(jnp.float32)
        forward.append(solved)
        if section + 1 < tile_count:
            pair_index = np.array(
                [tile * (tile - 1) // 2 + section for tile in range(section + 1, tile_count)],
                dtype=np.int32,
            )
            projections = jnp.einsum(
                "nw,mwr->mnr",
                solved.astype(jnp.bfloat16),
                low_right[pair_index],
                preferred_element_type=jnp.float32,
            )
            leading = lax.psum(projections[:1].astype(jnp.bfloat16), "col").astype(jnp.float32)
            if section + 2 < tile_count:
                remaining = lax.psum(projections[1:].astype(jnp.bfloat16), "col").astype(
                    jnp.float32
                )
                summed = jnp.concatenate([leading, remaining], axis=0)
            else:
                summed = leading
            masked = (summed * rank_mask(low_ranks, pair_index, rank_cols)[:, None, :]).astype(
                jnp.bfloat16
            )
            update = jnp.einsum(
                "mnr,mwr->mnw", masked, low_left[pair_index], preferred_element_type=jnp.float32
            )
            residual = residual.at[section + 1 :].add(-update)
    state = jnp.stack(forward)
    solutions = [None] * tile_count
    for section in range(tile_count - 1, -1, -1):
        rounded = state[section].astype(jnp.bfloat16)
        whole = lax.all_gather(rounded, "col", axis=1, tiled=True)
        moved = lax.all_to_all(whole, "row", split_axis=1, concat_axis=0, tiled=True)
        solved = lax.psum_scatter(
            sum_terms(moved, inv_upper[section]).astype(jnp.bfloat16),
            "row",
            scatter_dimension=0,
            tiled=True,
        ).astype(jnp.float32)
        solutions[section] = solved
        if section > 0:
            pair_index = np.array(
                [section * (section - 1) // 2 + tile for tile in range(section)], dtype=np.int32
            )
            projections = jnp.einsum(
                "nw,mwr->mnr",
                solved.astype(jnp.bfloat16),
                up_right[pair_index],
                preferred_element_type=jnp.float32,
            )
            leading = lax.psum(projections[-1:].astype(jnp.bfloat16), "col").astype(jnp.float32)
            if section > 1:
                remaining = lax.psum(projections[:-1].astype(jnp.bfloat16), "col").astype(
                    jnp.float32
                )
                summed = jnp.concatenate([remaining, leading], axis=0)
            else:
                summed = leading
            masked = (summed * rank_mask(up_ranks, pair_index, rank_cols)[:, None, :]).astype(
                jnp.bfloat16
            )
            update = jnp.einsum(
                "mnr,mwr->mnw", masked, up_left[pair_index], preferred_element_type=jnp.float32
            )
            state = state.at[:section].add(-update)
    return jnp.stack(solutions)


def solution(mesh):
    in_specs = (
        P(None, "row", "col"),
        P(None, "col", None),
        P(None, "col", None),
        P(None, "col", None),
        P(None, "col", None),
        P(),
        P(),
        P(None, "col", "row"),
        P(None, "col", "row"),
    )
    out_specs = P(None, "row", "col")
    return jax.shard_map(shards, mesh=mesh, in_specs=in_specs, out_specs=out_specs, check_vma=False)
```

profile of v0, /device:TPU:0, one launch (start us, length us, event | category | flops | bytes accessed | tf_op | source)
XLA Modules:
  0.0 1013.5 jit_solution(5519528377490401830)
XLA Ops:
  8.5 29.9 %all-gather.18.cloned.1.call-done = bf16[1,128,4096]{1,2,0:T(8,128)(2,1)} async-done(((bf16[1,128,1024]{1,2,0:T(8,128)(2,1)}), bf16[1,128,4096]{1,2,0:T(8,128)(2,1)}) %all-gather.18.cloned.1.call-update) | async-done | bytes 1048592 | tf_op jit(solution)/shard_map/all_gather | solution.py:34
  38.4 31.2 %all_to_all.152 = bf16[128,8,512]{0,2,1:T(8,128)(2,1)S(1)} all-to-all(bf16[128,8,512]{0,2,1:T(8,128)(2,1)} %bitcast.171), channel_id=1, replica_groups=mesh['row'=8,'col'=4] {'row'}, dimensions={1} | all-to-all | bytes 2097152 | tf_op jit(solution)/shard_map/all_to_all | solution.py:35
  70.1 3.8 convolution_convert_fusion.7
  76.8 31.4 %reduce-scatter.9.cloned.1.call-done = bf16[128,1024]{1,0:T(8,128)(2,1)} async-done(((bf16[1024,1024]{1,0:T(8,128)(2,1)}), bf16[128,1024]{1,0:T(8,128)(2,1)}) %reduce-scatter.9.cloned.1.call-update) | async-done | bytes 262160 | tf_op jit(solution)/shard_map/reduce_scatter | solution.py:36
  111.1 16.1 %psum.70 = bf16[1,128,128]{1,2,0:T(8,128)(2,1)S(1)} all-reduce(bf16[1,128,128]{1,2,0:T(8,128)(2,1)S(1)} %slice.332), channel_id=1, replica_groups=mesh['row'=8,'col'=4] {'col'}, use_global_device_ids=true, to_apply=%region_1.0 | all-reduce | flops 16384 | bytes 65536 | tf_op jit(solution)/shard_map/psum | solution.py:54
  127.2 24.3 %all-reduce.7.cloned.1.call-done = bf16[2,128,128]{1,2,0:T(8,128)(2,1)} async-done(((bf16[2,128,128]{1,2,0:T(8,128)(2,1)}), bf16[2,128,128]{1,2,0:T(8,128)(2,1)}) %all-reduce.7.cloned.1.call-update) | async-done | bytes 65552 | tf_op jit(solution)/shard_map/psum | solution.py:56
  151.5 2.0 negate_add_fusion.1
  154.2 26.6 %all-gather.20.cloned.1.call-done = bf16[1,128,4096]{2,1,0:T(8,128)(2,1)} async-done(((bf16[1,128,1024]{2,1,0:T(8,128)(2,1)}), bf16[1,128,4096]{2,1,0:T(8,128)(2,1)}) %all-gather.20.cloned.1.call-update) | async-done | bytes 1048592 | tf_op jit(solution)/shard_map/all_gather | solution.py:34
  182.8 31.0 %all_to_all.153 = bf16[128,8,512]{2,0,1:T(8,128)(2,1)S(1)} all-to-all(bf16[128,8,512]{2,0,1:T(8,128)(2,1)S(1)} %copy.61), channel_id=1, replica_groups=mesh['row'=8,'col'=4] {'row'}, dimensions={1} | all-to-all | bytes 2097152 | tf_op jit(solution)/shard_map/all_to_all | solution.py:35
  213.8 3.8 convolution_convert_fusion.6
  218.2 2.1 gather_fusion.3
  220.9 30.8 %reduce-scatter.11.cloned.1.call-done = bf16[128,1024]{1,0:T(8,128)(2,1)} async-done(((bf16[1024,1024]{1,0:T(8,128)(2,1)}), bf16[128,1024]{1,0:T(8,128)(2,1)}) %reduce-scatter.11.cloned.1.call-update) | async-done | bytes 262160 | tf_op jit(solution)/shard_map/reduce_scatter | solution.py:36
  253.9 2.1 gather_fusion.5
  255.9 39.0 %all-reduce.13.cloned.1.call-done = (bf16[1,128,128]{1,2,0:T(8,128)(2,1)}, bf16[1,128,128]{1,2,0:T(8,128)(2,1)}) async-done(((bf16[1,128,128]{1,2,0:T(8,128)(2,1)}, bf16[1,128,128]{1,2,0:T(8,128)(2,1)}), (bf16[1,128,128]{1,2,0:T(8,128)(2,1)}, bf16[1,128,128]{1,2,0:T(8,128)(2,1)})) %all-reduce.13.cloned.1.call-update) | async-done | bytes 65552 | tf_op jit(solution)/shard_map/psum | solution.py:56
  297.0 26.6 %all-gather.22.cloned.1.call-done = bf16[1,128,4096]{2,1,0:T(8,128)(2,1)} async-done(((bf16[1,128,1024]{2,1,0:T(8,128)(2,1)}), bf16[1,128,4096]{2,1,0:T(8,128)(2,1)}) %all-gather.22.cloned.1.call-update) | async-done | bytes 1048592 | tf_op jit(solution)/shard_map/all_gather | solution.py:34
  325.5 31.0 %all_to_all.154 = bf16[128,8,512]{2,0,1:T(8,128)(2,1)S(1)} all-to-all(bf16[128,8,512]{2,0,1:T(8,128)(2,1)S(1)} %copy.64), channel_id=1, replica_groups=mesh['row'=8,'col'=4] {'row'}, dimensions={1} | all-to-all | bytes 2097152 | tf_op jit(solution)/shard_map/all_to_all | solution.py:35
  356.5 3.8 convolution_convert_fusion.5
  361.6 32.9 %reduce-scatter.13.cloned.1.call-done = bf16[128,1024]{1,0:T(8,128)(2,1)} async-done(((bf16[1024,1024]{1,0:T(8,128)(2,1)}), bf16[128,1024]{1,0:T(8,128)(2,1)}) %reduce-scatter.13.cloned.1.call-update) | async-done | bytes 262160 | tf_op jit(solution)/shard_map/reduce_scatter | solution.py:36
  395.8 16.2 %psum.74 = bf16[1,128,128]{2,1,0:T(8,128)(2,1)S(1)} all-reduce(bf16[1,128,128]{2,1,0:T(8,128)(2,1)S(1)} %fusion.12), channel_id=1, replica_groups=mesh['row'=8,'col'=4] {'col'}, use_global_device_ids=true, to_apply=%region_7.0 | all-reduce | flops 16384 | bytes 65536 | tf_op jit(solution)/shard_map/psum | solution.py:54
  412.0 1.9 fusion.7
  414.0 23.0 %all-gather.24.cloned.1.call-done = bf16[1,128,4096]{2,1,0:T(8,128)(2,1)} async-done(((bf16[1,128,1024]{2,1,0:T(8,128)(2,1)}), bf16[1,128,4096]{2,1,0:T(8,128)(2,1)}) %all-gather.24.cloned.1.call-update) | async-done | bytes 1048592 | tf_op jit(solution)/shard_map/all_gather | solution.py:34
  438.9 31.0 %all_to_all.155 = bf16[128,8,512]{2,0,1:T(8,128)(2,1)S(1)} all-to-all(bf16[128,8,512]{2,0,1:T(8,128)(2,1)S(1)} %copy.65), channel_id=1, replica_groups=mesh['row'=8,'col'=4] {'row'}, dimensions={1} | all-to-all | bytes 2097152 | tf_op jit(solution)/shard_map/all_to_all | solution.py:35
  469.9 3.8 convolution_convert_fusion.4
  473.8 34.1 %reduce-scatter.15.cloned.1.call-done = bf16[128,1024]{1,0:T(8,128)(2,1)} async-done(((bf16[1024,1024]{1,0:T(8,128)(2,1)}), bf16[128,1024]{1,0:T(8,128)(2,1)}) %reduce-scatter.15.cloned.1.call-update) | async-done | bytes 262160 | tf_op jit(solution)/shard_map/reduce_scatter | solution.py:36
  508.0 26.8 %all-gather.16.cloned.1.call-done = bf16[128,4096]{1,0:T(8,128)(2,1)} async-done(((bf16[128,1024]{1,0:T(8,128)(2,1)}), bf16[128,4096]{1,0:T(8,128)(2,1)}) %all-gather.16.cloned.1.call-update) | async-done | bytes 1048592 | tf_op jit(solution)/shard_map/all_gather | solution.py:73
  536.1 31.0 %all_to_all.156 = bf16[128,8,512]{2,0,1:T(8,128)(2,1)S(1)} all-to-all(bf16[128,8,512]{2,0,1:T(8,128)(2,1)S(1)} %bitcast.165), channel_id=1, replica_groups=mesh['row'=8,'col'=4] {'row'}, dimensions={1} | all-to-all | bytes 2097152 | tf_op jit(solution)/shard_map/all_to_all | solution.py:74
  567.1 3.8 convolution_convert_fusion.3
  573.8 31.4 %reduce-scatter.17.cloned.1.call-done = bf16[128,1024]{1,0:T(8,128)(2,1)} async-done(((bf16[1024,1024]{1,0:T(8,128)(2,1)}), bf16[128,1024]{1,0:T(8,128)(2,1)}) %reduce-scatter.17.cloned.1.call-update) | async-done | bytes 262160 | tf_op jit(solution)/shard_map/reduce_scatter | solution.py:75
  608.0 16.3 %psum.76 = bf16[1,128,128]{1,2,0:T(8,128)(2,1)S(1)} all-reduce(bf16[1,128,128]{1,2,0:T(8,128)(2,1)S(1)} %slice.341), channel_id=1, replica_groups=mesh['row'=8,'col'=4] {'col'}, use_global_device_ids=true, to_apply=%region_11.0 | all-reduce | flops 16384 | bytes 65536 | tf_op jit(solution)/shard_map/psum | solution.py:92
  624.3 24.1 %all-reduce.9.cloned.1.call-done = bf16[2,128,128]{1,2,0:T(8,128)(2,1)} async-done(((bf16[2,128,128]{1,2,0:T(8,128)(2,1)}), bf16[2,128,128]{1,2,0:T(8,128)(2,1)}) %all-reduce.9.cloned.1.call-update) | async-done | bytes 65552 | tf_op jit(solution)/shard_map/psum | solution.py:94
  650.6 26.6 %all-gather.26.cloned.1.call-done = bf16[1,128,4096]{2,1,0:T(8,128)(2,1)} async-done(((bf16[1,128,1024]{2,1,0:T(8,128)(2,1)}), bf16[1,128,4096]{2,1,0:T(8,128)(2,1)}) %all-gather.26.cloned.1.call-update) | async-done | bytes 1048592 | tf_op jit(solution)/shard_map/all_gather | solution.py:73
  679.1 31.0 %all_to_all.157 = bf16[128,8,512]{2,0,1:T(8,128)(2,1)S(1)} all-to-all(bf16[128,8,512]{2,0,1:T(8,128)(2,1)S(1)} %copy.69), channel_id=1, replica_groups=mesh['row'=8,'col'=4] {'row'}, dimensions={1} | all-to-all | bytes 2097152 | tf_op jit(solution)/shard_map/all_to_all | solution.py:74
  710.1 3.8 convolution_convert_fusion.2
  714.6 2.1 gather_fusion.9
  717.3 30.9 %reduce-scatter.19.cloned.1.call-done = bf16[128,1024]{1,0:T(8,128)(2,1)} async-done(((bf16[1024,1024]{1,0:T(8,128)(2,1)}), bf16[128,1024]{1,0:T(8,128)(2,1)}) %reduce-scatter.19.cloned.1.call-update) | async-done | bytes 262160 | tf_op jit(solution)/shard_map/reduce_scatter | solution.py:75
  750.2 2.1 gather_fusion.11
  752.3 39.0 %all-reduce.11.cloned.1.call-done = (bf16[1,128,128]{1,2,0:T(8,128)(2,1)}, bf16[1,128,128]{1,2,0:T(8,128)(2,1)}) async-done(((bf16[1,128,128]{1,2,0:T(8,128)(2,1)}, bf16[1,128,128]{1,2,0:T(8,128)(2,1)}), (bf16[1,128,128]{1,2,0:T(8,128)(2,1)}, bf16[1,128,128]{1,2,0:T(8,128)(2,1)})) %all-reduce.11.cloned.1.call-update) | async-done | bytes 65552 | tf_op jit(solution)/shard_map/psum | solution.py:92
  793.3 26.6 %all-gather.28.cloned.1.call-done = bf16[1,128,4096]{2,1,0:T(8,128)(2,1)} async-done(((bf16[1,128,1024]{2,1,0:T(8,128)(2,1)}), bf16[1,128,4096]{2,1,0:T(8,128)(2,1)}) %all-gather.28.cloned.1.call-update) | async-done | bytes 1048592 | tf_op jit(solution)/shard_map/all_gather | solution.py:73
  821.8 31.0 %all_to_all.158 = bf16[128,8,512]{2,0,1:T(8,128)(2,1)S(1)} all-to-all(bf16[128,8,512]{2,0,1:T(8,128)(2,1)S(1)} %copy.72), channel_id=1, replica_groups=mesh['row'=8,'col'=4] {'row'}, dimensions={1} | all-to-all | bytes 2097152 | tf_op jit(solution)/shard_map/all_to_all | solution.py:74
  852.8 3.8 convolution_convert_fusion.1
  856.7 34.1 %reduce-scatter.21.cloned.1.call-done = bf16[128,1024]{1,0:T(8,128)(2,1)} async-done(((bf16[1024,1024]{1,0:T(8,128)(2,1)}), bf16[128,1024]{1,0:T(8,128)(2,1)}) %reduce-scatter.21.cloned.1.call-update) | async-done | bytes 262160 | tf_op jit(solution)/shard_map/reduce_scatter | solution.py:75
  892.0 16.2 %psum.79 = bf16[1,128,128]{2,1,0:T(8,128)(2,1)S(1)} all-reduce(bf16[1,128,128]{2,1,0:T(8,128)(2,1)S(1)} %fusion.13), channel_id=1, replica_groups=mesh['row'=8,'col'=4] {'col'}, use_global_device_ids=true, to_apply=%region_16.0 | all-reduce | flops 16384 | bytes 65536 | tf_op jit(solution)/shard_map/psum | solution.py:92
  908.2 1.9 fusion.6
  910.2 23.0 %all-gather.30.cloned.1.call-done = bf16[1,128,4096]{2,1,0:T(8,128)(2,1)} async-done(((bf16[1,128,1024]{2,1,0:T(8,128)(2,1)}), bf16[1,128,4096]{2,1,0:T(8,128)(2,1)}) %all-gather.30.cloned.1.call-update) | async-done | bytes 1048592 | tf_op jit(solution)/shard_map/all_gather | solution.py:73
  935.1 31.0 %all_to_all.159 = bf16[128,8,512]{2,0,1:T(8,128)(2,1)S(1)} all-to-all(bf16[128,8,512]{2,0,1:T(8,128)(2,1)S(1)} %copy.73), channel_id=1, replica_groups=mesh['row'=8,'col'=4] {'row'}, dimensions={1} | all-to-all | bytes 2097152 | tf_op jit(solution)/shard_map/all_to_all | solution.py:74
  966.1 3.8 convolution_convert_fusion
  970.0 34.2 %reduce-scatter.23.cloned.1.call-done = bf16[128,1024]{1,0:T(8,128)(2,1)} async-done(((bf16[1024,1024]{1,0:T(8,128)(2,1)}), bf16[128,1024]{1,0:T(8,128)(2,1)}) %reduce-scatter.23.cloned.1.call-update) | async-done | bytes 262160 | tf_op jit(solution)/shard_map/reduce_scatter | solution.py:75
  1004.2 2.4 maximum_convert_fusion
  (130 shorter events, 43.7 us)
Async XLA Ops:
  6.5 31.9 %all-gather.18.cloned.1.call-start = ((), (), s32[]{:S(2)}) async-start(), calls=%async_computation.27 | async-start | bytes 1310720 | tf_op jit(solution)/shard_map/all_gather | solution.py:34
  8.5 99.7 %reduce-scatter.9.cloned.1.call-start = ((), (), s32[]{:S(2)}) async-start(), calls=%async_computation.16 | async-start | bytes 2359296 | tf_op jit(solution)/shard_map/reduce_scatter | solution.py:36
  74.0 0.7 copy-start.15
  74.0 1.4 copy-start.2
  74.0 2.1 copy-start
  74.0 77.5 %all-reduce.7.cloned.1.call-start = ((), (), s32[]{:S(2)}) async-start(), calls=%async_computation.17 | async-start | bytes 131072 | tf_op jit(solution)/shard_map/psum | solution.py:56
  76.1 34.2 %copy-start.4 = (bf16[6,1024,128]{2,1,0:T(8,128)(2,1)S(1)}, bf16[6,1024,128]{2,1,0:T(8,128)(2,1)}, u32[]{:S(2)}) copy-start(bf16[6,1024,128]{2,1,0:T(8,128)(2,1)} %param.46) | copy-start | bytes 4718596
  110.2 70.6 %all-gather.20.cloned.1.call-start = ((), (), s32[]{:S(2)}) async-start(), calls=%async_computation.28 | async-start | bytes 1310720 | tf_op jit(solution)/shard_map/all_gather | solution.py:34
  154.2 97.6 %reduce-scatter.11.cloned.1.call-start = ((), (), s32[]{:S(2)}) async-start(), calls=%async_computation.18 | async-start | bytes 2359296 | tf_op jit(solution)/shard_map/reduce_scatter | solution.py:36
  217.6 0.7 copy-start.14
  217.6 77.3 %all-reduce.13.cloned.1.call-start = ((), (), s32[]{:S(2)}) async-start(), calls=%async_computation.35 | async-start | bytes 131072 | tf_op jit(solution)/shard_map/psum | solution.py:56
  253.7 69.8 %all-gather.22.cloned.1.call-start = ((), (), s32[]{:S(2)}) async-start(), calls=%async_computation.29 | async-start | bytes 1310720 | tf_op jit(solution)/shard_map/all_gather | solution.py:34
  296.9 97.6 %reduce-scatter.13.cloned.1.call-start = ((), (), s32[]{:S(2)}) async-start(), calls=%async_computation.19 | async-start | bytes 2359296 | tf_op jit(solution)/shard_map/reduce_scatter | solution.py:36
  360.3 76.7 %all-gather.24.cloned.1.call-start = ((), (), s32[]{:S(2)}) async-start(), calls=%async_computation.30 | async-start | bytes 1310720 | tf_op jit(solution)/shard_map/all_gather | solution.py:34
  413.9 94.0 %reduce-scatter.15.cloned.1.call-start = ((), (), s32[]{:S(2)}) async-start(), calls=%async_computation.20 | async-start | bytes 2359296 | tf_op jit(solution)/shard_map/reduce_scatter | solution.py:36
  473.8 61.0 %all-gather.16.cloned.1.call-start = ((), (), s32[]{:S(2)}) async-start(), calls=%async_computation.21 | async-start | bytes 1310720 | tf_op jit(solution)/shard_map/all_gather | solution.py:73
  508.0 97.2 %reduce-scatter.17.cloned.1.call-start = ((), (), s32[]{:S(2)}) async-start(), calls=%async_computation.22 | async-start | bytes 2359296 | tf_op jit(solution)/shard_map/reduce_scatter | solution.py:75
  570.9 0.7 copy-start.13
  570.9 1.4 copy-start.3
  570.9 2.1 copy-start.1
  571.0 77.4 %all-reduce.9.cloned.1.call-start = ((), (), s32[]{:S(2)}) async-start(), calls=%async_computation.23 | async-start | bytes 131072 | tf_op jit(solution)/shard_map/psum | solution.py:94
  573.1 34.2 %copy-start.5 = (bf16[6,1024,128]{2,1,0:T(8,128)(2,1)S(1)}, bf16[6,1024,128]{2,1,0:T(8,128)(2,1)}, u32[]{:S(2)}) copy-start(bf16[6,1024,128]{2,1,0:T(8,128)(2,1)} %param.48) | copy-start | bytes 4718596
  573.1 75.3 %copy-start.9 = (bf16[128,1024]{1,0:T(8,128)(2,1)S(1)}, bf16[128,1024]{1,0:T(8,128)(2,1)}, u32[]{:S(2)}) copy-start(bf16[128,1024]{1,0:T(8,128)(2,1)} %reduce-scatter.11.cloned.1.call-done) | copy-start | bytes 786436
  573.1 75.3 %copy-start.10 = (bf16[128,1024]{1,0:T(8,128)(2,1)S(1)}, bf16[128,1024]{1,0:T(8,128)(2,1)}, u32[]{:S(2)}) copy-start(bf16[128,1024]{1,0:T(8,128)(2,1)} %reduce-scatter.13.cloned.1.call-done) | copy-start | bytes 786436
  573.1 75.3 %copy-start.11 = (bf16[128,1024]{1,0:T(8,128)(2,1)S(1)}, bf16[128,1024]{1,0:T(8,128)(2,1)}, u32[]{:S(2)}) copy-start(bf16[128,1024]{1,0:T(8,128)(2,1)} %reduce-scatter.9.cloned.1.call-done) | copy-start | bytes 786436
  607.2 70.0 %all-gather.26.cloned.1.call-start = ((), (), s32[]{:S(2)}) async-start(), calls=%async_computation.31 | async-start | bytes 1310720 | tf_op jit(solution)/shard_map/all_gather | solution.py:73
  650.5 97.6 %reduce-scatter.19.cloned.1.call-start = ((), (), s32[]{:S(2)}) async-start(), calls=%async_computation.24 | async-start | bytes 2359296 | tf_op jit(solution)/shard_map/reduce_scatter | solution.py:75
  713.9 0.7 copy-start.12
  713.9 77.3 %all-reduce.11.cloned.1.call-start = ((), (), s32[]{:S(2)}) async-start(), calls=%async_computation.34 | async-start | bytes 131072 | tf_op jit(solution)/shard_map/psum | solution.py:92
  750.1 69.8 %all-gather.28.cloned.1.call-start = ((), (), s32[]{:S(2)}) async-start(), calls=%async_computation.32 | async-start | bytes 1310720 | tf_op jit(solution)/shard_map/all_gather | solution.py:73
  793.2 97.6 %reduce-scatter.21.cloned.1.call-start = ((), (), s32[]{:S(2)}) async-start(), calls=%async_computation.25 | async-start | bytes 2359296 | tf_op jit(solution)/shard_map/reduce_scatter | solution.py:75
  856.6 76.6 %all-gather.30.cloned.1.call-start = ((), (), s32[]{:S(2)}) async-start(), calls=%async_computation.33 | async-start | bytes 1310720 | tf_op jit(solution)/shard_map/all_gather | solution.py:73
  910.1 94.0 %reduce-scatter.23.cloned.1.call-start = ((), (), s32[]{:S(2)}) async-start(), calls=%async_computation.26 | async-start | bytes 2359296 | tf_op jit(solution)/shard_map/reduce_scatter | solution.py:75
  969.9 34.2 %copy-start.6 = (bf16[128,1024]{1,0:T(8,128)(2,1)S(1)}, bf16[128,1024]{1,0:T(8,128)(2,1)}, u32[]{:S(2)}) copy-start(bf16[128,1024]{1,0:T(8,128)(2,1)} %reduce-scatter.19.cloned.1.call-done) | copy-start | bytes 786436
  969.9 34.2 %copy-start.7 = (bf16[128,1024]{1,0:T(8,128)(2,1)S(1)}, bf16[128,1024]{1,0:T(8,128)(2,1)}, u32[]{:S(2)}) copy-start(bf16[128,1024]{1,0:T(8,128)(2,1)} %reduce-scatter.21.cloned.1.call-done) | copy-start | bytes 786436
  969.9 34.2 %copy-start.8 = (bf16[128,1024]{1,0:T(8,128)(2,1)S(1)}, bf16[128,1024]{1,0:T(8,128)(2,1)}, u32[]{:S(2)}) copy-start(bf16[128,1024]{1,0:T(8,128)(2,1)} %reduce-scatter.17.cloned.1.call-done) | copy-start | bytes 786436
Sparse Core Ops, SparseCore 0:
  9.2 29.2 all-gather.17
  74.1 34.0 reduce-scatter.8
  111.1 40.3 all-reduce.6
  154.3 26.4 all-gather.19
  217.7 34.0 reduce-scatter.10
  254.5 40.4 all-reduce.12
  297.0 26.4 all-gather.21
  360.4 34.0 reduce-scatter.12
  414.1 22.9 all-gather.23
  473.9 34.0 reduce-scatter.14
  509.8 24.9 all-gather.15
  571.1 34.0 reduce-scatter.16
  608.0 40.3 all-reduce.8
  650.7 26.4 all-gather.25
  714.1 34.0 reduce-scatter.18
  750.8 40.3 all-reduce.10
  793.3 26.4 all-gather.27
  856.8 34.0 reduce-scatter.20
  910.3 22.8 all-gather.29
  970.1 34.0 reduce-scatter.22
where the time goes:
time: 1020 us; the launch traced here: 1010 us
  waiting for transfers between devices  596 us (58%)
  blocking collectives  313 us (31%)
  matrix products  47.9 us (5%)
  local copies, waits for them, and re-layouts  38.9 us (4%)
  between operations  14.7 us (1%)
    all_to_all x8, blocking collectives, shards(): lax.all_to_all(whole, 'row', split_axis=1, concat_axis=0, tiled=True)  248 us
    all_gather x8, waiting for transfers between devices, shards(): whole = lax.all_gather(rounded, 'col', axis=1, tiled=True)  209 us
    reduce_scatter x4, waiting for transfers between devices, shards(): lax.psum_scatter(sum_terms(moved, inv_upper[section]).astype(jnp.bfloat16...  130 us
    reduce_scatter x4, waiting for transfers between devices, shards(): lax.psum_scatter(sum_terms(moved, inv_lower[section]).astype(jnp.bfloat16...  129 us
    psum x2, waiting for transfers between devices, shards(): lax.psum(projections[1:].astype(jnp.bfloat16), 'col').astype(jnp.float32)  63.3 us
    psum x1, waiting for transfers between devices, shards(): lax.psum(projections[-1:].astype(jnp.bfloat16), 'col').astype(jnp.float32)  39 us
    psum x2, blocking collectives, shards(): lax.psum(projections[-1:].astype(jnp.bfloat16), 'col').astype(jnp.float32)  32.5 us
    psum x2, blocking collectives, shards(): lax.psum(projections[:1].astype(jnp.bfloat16), 'col').astype(jnp.float32)  32.4 us
  transfers between devices with their start and end apart: 20, of which 20 were waited for; matrix products, arithmetic and copies ran while one was open for 1% of the time, Pallas kernels for 0%

commit v1 on v0

--- a/solution.py
+++ b/solution.py
@@ -31,7 +31,7 @@
     forward = []
     for section in range(tile_count):
         rounded = residual[section].astype(jnp.bfloat16)
-        whole = lax.all_gather(rounded, "col", axis=1, tiled=True)
+        whole = jnp.concatenate(lax.all_gather(rounded, "col"), axis=1)
         moved = lax.all_to_all(whole, "row", split_axis=1, concat_axis=0, tiled=True)
         solved = lax.psum_scatter(
             sum_terms(moved, inv_lower[section]).astype(jnp.bfloat16),

time: 1020 us -> 1020 us (level)
    all_gather x0 -> x4, waiting for transfers between devices: none -> 106 us  [shards(): whole = jnp.concatenate(lax.all_gather(rounded, 'col'), axis=1)]
    all_gather x8 -> x4, waiting for transfers between devices: 209 us -> 103 us  [shards(): whole = lax.all_gather(rounded, 'col', axis=1, tiled=True)]
  transfers between devices with their start and end apart: 20 -> 20, of which waited for: 20 -> 20; matrix products, arithmetic and copies ran while one was open for 1% -> 2% of each run, Pallas kernels for 0% -> 0%
where the time goes in v1:
time: 1020 us
  waiting for transfers between devices  593 us (58%)
  blocking collectives  313 us (31%)
  matrix products  47.9 us (5%)
  local copies, waits for them, and re-layouts  44.8 us (4%)
  between operations  14.8 us (1%)
    all_to_all x8, blocking collectives, shards(): lax.all_to_all(whole, 'row', split_axis=1, concat_axis=0, tiled=True)  248 us
    reduce_scatter x4, waiting for transfers between devices, shards(): lax.psum_scatter(sum_terms(moved, inv_upper[section]).astype(jnp.bfloat16...  130 us
    reduce_scatter x4, waiting for transfers between devices, shards(): lax.psum_scatter(sum_terms(moved, inv_lower[section]).astype(jnp.bfloat16...  129 us
    all_gather x4, waiting for transfers between devices, shards(): whole = jnp.concatenate(lax.all_gather(rounded, 'col'), axis=1)  106 us
    all_gather x4, waiting for transfers between devices, shards(): whole = lax.all_gather(rounded, 'col', axis=1, tiled=True)  103 us
    psum x2, waiting for transfers between devices, shards(): lax.psum(projections[1:].astype(jnp.bfloat16), 'col').astype(jnp.float32)  61.9 us
    psum x1, waiting for transfers between devices, shards(): lax.psum(projections[-1:].astype(jnp.bfloat16), 'col').astype(jnp.float32)  39 us
    psum x2, blocking collectives, shards(): lax.psum(projections[:1].astype(jnp.bfloat16), 'col').astype(jnp.float32)  32.5 us
  transfers between devices with their start and end apart: 20, of which 20 were waited for; matrix products, arithmetic and copies ran while one was open for 2% of the time, Pallas kernels for 0%

profile of v1, /device:TPU:0, one launch (start us, length us, event | category | flops | bytes accessed | tf_op | source)
XLA Modules:
  0.0 1016.8 jit_solution(6012802520915342633)
XLA Ops:
  8.4 30.0 %all-gather.12.cloned.1.call-done = bf16[4,128,1024]{2,1,0:T(8,128)(2,1)} async-done(((bf16[1,128,1024]{2,1,0:T(8,128)(2,1)}), bf16[4,128,1024]{2,1,0:T(8,128)(2,1)}) %all-gather.12.cloned.1.call-update) | async-done | bytes 1048592 | tf_op jit(solution)/shard_map/all_gather | solution.py:34
  40.0 31.0 %all_to_all.152 = bf16[128,8,512]{0,2,1:T(8,128)(2,1)S(1)} all-to-all(bf16[128,8,512]{0,2,1:T(8,128)(2,1)S(1)} %bitcast.160), channel_id=1, replica_groups=mesh['row'=8,'col'=4] {'row'}, dimensions={1} | all-to-all | bytes 2097152 | tf_op jit(solution)/shard_map/all_to_all | solution.py:35
  71.5 3.8 convolution_convert_fusion.7
  78.2 31.4 %reduce-scatter.9.cloned.1.call-done = bf16[128,1024]{1,0:T(8,128)(2,1)} async-done(((bf16[1024,1024]{1,0:T(8,128)(2,1)}), bf16[128,1024]{1,0:T(8,128)(2,1)}) %reduce-scatter.9.cloned.1.call-update) | async-done | bytes 262160 | tf_op jit(solution)/shard_map/reduce_scatter | solution.py:36
  111.7 2.1 gather_fusion.2
  113.9 16.2 %psum.70 = bf16[1,128,128]{1,2,0:T(8,128)(2,1)S(1)} all-reduce(bf16[1,128,128]{1,2,0:T(8,128)(2,1)S(1)} %slice.332), channel_id=1, replica_groups=mesh['row'=8,'col'=4] {'col'}, use_global_device_ids=true, to_apply=%region_1.0 | all-reduce | flops 16384 | bytes 65536 | tf_op jit(solution)/shard_map/psum | solution.py:54
  130.1 22.8 %all-reduce.7.cloned.1.call-done = bf16[2,128,128]{1,2,0:T(8,128)(2,1)} async-done(((bf16[2,128,128]{1,2,0:T(8,128)(2,1)}), bf16[2,128,128]{1,2,0:T(8,128)(2,1)}) %all-reduce.7.cloned.1.call-update) | async-done | bytes 65552 | tf_op jit(solution)/shard_map/psum | solution.py:56
  152.8 2.0 negate_add_fusion.1
  155.6 26.6 %all-gather.14.cloned.1.call-done = bf16[4,128,1024]{2,1,0:T(8,128)(2,1)} async-done(((bf16[1,128,1024]{2,1,0:T(8,128)(2,1)}), bf16[4,128,1024]{2,1,0:T(8,128)(2,1)}) %all-gather.14.cloned.1.call-update) | async-done | bytes 1048592 | tf_op jit(solution)/shard_map/all_gather | solution.py:34
  183.9 31.1 %all_to_all.153 = bf16[128,8,512]{0,2,1:T(8,128)(2,1)} all-to-all(bf16[128,8,512]{0,2,1:T(8,128)(2,1)S(1)} %bitcast.162), channel_id=1, replica_groups=mesh['row'=8,'col'=4] {'row'}, dimensions={1} | all-to-all | bytes 2097152 | tf_op jit(solution)/shard_map/all_to_all | solution.py:35
  216.4 3.8 convolution_convert_fusion.6
  220.9 2.1 gather_fusion.3
  223.6 30.8 %reduce-scatter.11.cloned.1.call-done = bf16[128,1024]{1,0:T(8,128)(2,1)} async-done(((bf16[1024,1024]{1,0:T(8,128)(2,1)}), bf16[128,1024]{1,0:T(8,128)(2,1)}) %reduce-scatter.11.cloned.1.call-update) | async-done | bytes 262160 | tf_op jit(solution)/shard_map/reduce_scatter | solution.py:36
  256.5 2.1 gather_fusion.5
  258.6 39.1 %all-reduce.13.cloned.1.call-done = (bf16[1,128,128]{1,2,0:T(8,128)(2,1)}, bf16[1,128,128]{1,2,0:T(8,128)(2,1)}) async-done(((bf16[1,128,128]{1,2,0:T(8,128)(2,1)}, bf16[1,128,128]{1,2,0:T(8,128)(2,1)}), (bf16[1,128,128]{1,2,0:T(8,128)(2,1)}, bf16[1,128,128]{1,2,0:T(8,128)(2,1)})) %all-reduce.13.cloned.1.call-update) | async-done | bytes 65552 | tf_op jit(solution)/shard_map/psum | solution.py:56
  299.7 26.6 %all-gather.16.cloned.1.call-done = bf16[4,128,1024]{2,1,0:T(8,128)(2,1)} async-done(((bf16[1,128,1024]{2,1,0:T(8,128)(2,1)}), bf16[4,128,1024]{2,1,0:T(8,128)(2,1)}) %all-gather.16.cloned.1.call-update) | async-done | bytes 1048592 | tf_op jit(solution)/shard_map/all_gather | solution.py:34
  328.0 31.0 %all_to_all.154 = bf16[128,8,512]{0,2,1:T(8,128)(2,1)S(1)} all-to-all(bf16[128,8,512]{0,2,1:T(8,128)(2,1)S(1)} %bitcast.164), channel_id=1, replica_groups=mesh['row'=8,'col'=4] {'row'}, dimensions={1} | all-to-all | bytes 2097152 | tf_op jit(solution)/shard_map/all_to_all | solution.py:35
  359.5 3.8 convolution_convert_fusion.5
  364.8 32.8 %reduce-scatter.13.cloned.1.call-done = bf16[128,1024]{1,0:T(8,128)(2,1)} async-done(((bf16[1024,1024]{1,0:T(8,128)(2,1)}), bf16[128,1024]{1,0:T(8,128)(2,1)}) %reduce-scatter.13.cloned.1.call-update) | async-done | bytes 262160 | tf_op jit(solution)/shard_map/reduce_scatter | solution.py:36
  398.8 16.3 %psum.74 = bf16[1,128,128]{2,1,0:T(8,128)(2,1)S(1)} all-reduce(bf16[1,128,128]{2,1,0:T(8,128)(2,1)S(1)} %fusion.12), channel_id=1, replica_groups=mesh['row'=8,'col'=4] {'col'}, use_global_device_ids=true, to_apply=%region_7.0 | all-reduce | flops 16384 | bytes 65536 | tf_op jit(solution)/shard_map/psum | solution.py:54
  417.1 22.9 %all-gather.18.cloned.1.call-done = bf16[4,128,1024]{2,1,0:T(8,128)(2,1)} async-done(((bf16[1,128,1024]{2,1,0:T(8,128)(2,1)}), bf16[4,128,1024]{2,1,0:T(8,128)(2,1)}) %all-gather.18.cloned.1.call-update) | async-done | bytes 1048592 | tf_op jit(solution)/shard_map/all_gather | solution.py:34
  441.7 31.0 %all_to_all.155 = bf16[128,8,512]{0,2,1:T(8,128)(2,1)S(1)} all-to-all(bf16[128,8,512]{0,2,1:T(8,128)(2,1)S(1)} %bitcast.166), channel_id=1, replica_groups=mesh['row'=8,'col'=4] {'row'}, dimensions={1} | all-to-all | bytes 2097152 | tf_op jit(solution)/shard_map/all_to_all | solution.py:35
  473.2 3.8 convolution_convert_fusion.4
  477.1 34.1 %reduce-scatter.15.cloned.1.call-done = bf16[128,1024]{1,0:T(8,128)(2,1)} async-done(((bf16[1024,1024]{1,0:T(8,128)(2,1)}), bf16[128,1024]{1,0:T(8,128)(2,1)}) %reduce-scatter.15.cloned.1.call-update) | async-done | bytes 262160 | tf_op jit(solution)/shard_map/reduce_scatter | solution.py:36
  511.3 26.8 %all-gather.20.cloned.1.call-done = bf16[128,4096]{1,0:T(8,128)(2,1)} async-done(((bf16[128,1024]{1,0:T(8,128)(2,1)}), bf16[128,4096]{1,0:T(8,128)(2,1)}) %all-gather.20.cloned.1.call-update) | async-done | bytes 1048592 | tf_op jit(solution)/shard_map/all_gather | solution.py:73
  539.4 31.0 %all_to_all.156 = bf16[128,8,512]{2,0,1:T(8,128)(2,1)S(1)} all-to-all(bf16[128,8,512]{2,0,1:T(8,128)(2,1)S(1)} %bitcast.168), channel_id=1, replica_groups=mesh['row'=8,'col'=4] {'row'}, dimensions={1} | all-to-all | bytes 2097152 | tf_op jit(solution)/shard_map/all_to_all | solution.py:74
  570.4 3.8 convolution_convert_fusion.3
  577.0 31.4 %reduce-scatter.17.cloned.1.call-done = bf16[128,1024]{1,0:T(8,128)(2,1)} async-done(((bf16[1024,1024]{1,0:T(8,128)(2,1)}), bf16[128,1024]{1,0:T(8,128)(2,1)}) %reduce-scatter.17.cloned.1.call-update) | async-done | bytes 262160 | tf_op jit(solution)/shard_map/reduce_scatter | solution.py:75
  610.8 2.1 gather_fusion.8
  612.9 16.2 %psum.76 = bf16[1,128,128]{1,2,0:T(8,128)(2,1)S(1)} all-reduce(bf16[1,128,128]{1,2,0:T(8,128)(2,1)S(1)} %slice.341), channel_id=1, replica_groups=mesh['row'=8,'col'=4] {'col'}, use_global_device_ids=true, to_apply=%region_11.0 | all-reduce | flops 16384 | bytes 65536 | tf_op jit(solution)/shard_map/psum | solution.py:92
  629.1 22.6 %all-reduce.9.cloned.1.call-done = bf16[2,128,128]{1,2,0:T(8,128)(2,1)} async-done(((bf16[2,128,128]{1,2,0:T(8,128)(2,1)}), bf16[2,128,128]{1,2,0:T(8,128)(2,1)}) %all-reduce.9.cloned.1.call-update) | async-done | bytes 65552 | tf_op jit(solution)/shard_map/psum | solution.py:94
  653.9 26.6 %all-gather.22.cloned.1.call-done = bf16[1,128,4096]{2,1,0:T(8,128)(2,1)} async-done(((bf16[1,128,1024]{2,1,0:T(8,128)(2,1)}), bf16[1,128,4096]{2,1,0:T(8,128)(2,1)}) %all-gather.22.cloned.1.call-update) | async-done | bytes 1048592 | tf_op jit(solution)/shard_map/all_gather | solution.py:73
  682.4 31.0 %all_to_all.157 = bf16[128,8,512]{2,0,1:T(8,128)(2,1)S(1)} all-to-all(bf16[128,8,512]{2,0,1:T(8,128)(2,1)S(1)} %copy.77), channel_id=1, replica_groups=mesh['row'=8,'col'=4] {'row'}, dimensions={1} | all-to-all | bytes 2097152 | tf_op jit(solution)/shard_map/all_to_all | solution.py:74
  713.4 3.8 convolution_convert_fusion.2
  717.9 2.1 gather_fusion.9
  720.6 30.8 %reduce-scatter.19.cloned.1.call-done = bf16[128,1024]{1,0:T(8,128)(2,1)} async-done(((bf16[1024,1024]{1,0:T(8,128)(2,1)}), bf16[128,1024]{1,0:T(8,128)(2,1)}) %reduce-scatter.19.cloned.1.call-update) | async-done | bytes 262160 | tf_op jit(solution)/shard_map/reduce_scatter | solution.py:75
  753.5 2.1 gather_fusion.11
  755.5 39.0 %all-reduce.11.cloned.1.call-done = (bf16[1,128,128]{1,2,0:T(8,128)(2,1)}, bf16[1,128,128]{1,2,0:T(8,128)(2,1)}) async-done(((bf16[1,128,128]{1,2,0:T(8,128)(2,1)}, bf16[1,128,128]{1,2,0:T(8,128)(2,1)}), (bf16[1,128,128]{1,2,0:T(8,128)(2,1)}, bf16[1,128,128]{1,2,0:T(8,128)(2,1)})) %all-reduce.11.cloned.1.call-update) | async-done | bytes 65552 | tf_op jit(solution)/shard_map/psum | solution.py:92
  796.6 26.6 %all-gather.24.cloned.1.call-done = bf16[1,128,4096]{2,1,0:T(8,128)(2,1)} async-done(((bf16[1,128,1024]{2,1,0:T(8,128)(2,1)}), bf16[1,128,4096]{2,1,0:T(8,128)(2,1)}) %all-gather.24.cloned.1.call-update) | async-done | bytes 1048592 | tf_op jit(solution)/shard_map/all_gather | solution.py:73
  825.1 31.0 %all_to_all.158 = bf16[128,8,512]{2,0,1:T(8,128)(2,1)S(1)} all-to-all(bf16[128,8,512]{2,0,1:T(8,128)(2,1)S(1)} %copy.80), channel_id=1, replica_groups=mesh['row'=8,'col'=4] {'row'}, dimensions={1} | all-to-all | bytes 2097152 | tf_op jit(solution)/shard_map/all_to_all | solution.py:74
  856.1 3.8 convolution_convert_fusion.1
  860.0 34.1 %reduce-scatter.21.cloned.1.call-done = bf16[128,1024]{1,0:T(8,128)(2,1)} async-done(((bf16[1024,1024]{1,0:T(8,128)(2,1)}), bf16[128,1024]{1,0:T(8,128)(2,1)}) %reduce-scatter.21.cloned.1.call-update) | async-done | bytes 262160 | tf_op jit(solution)/shard_map/reduce_scatter | solution.py:75
  895.4 16.2 %psum.79 = bf16[1,128,128]{2,1,0:T(8,128)(2,1)S(1)} all-reduce(bf16[1,128,128]{2,1,0:T(8,128)(2,1)S(1)} %fusion.13), channel_id=1, replica_groups=mesh['row'=8,'col'=4] {'col'}, use_global_device_ids=true, to_apply=%region_16.0 | all-reduce | flops 16384 | bytes 65536 | tf_op jit(solution)/shard_map/psum | solution.py:92
  913.5 23.0 %all-gather.26.cloned.1.call-done = bf16[1,128,4096]{2,1,0:T(8,128)(2,1)} async-done(((bf16[1,128,1024]{2,1,0:T(8,128)(2,1)}), bf16[1,128,4096]{2,1,0:T(8,128)(2,1)}) %all-gather.26.cloned.1.call-update) | async-done | bytes 1048592 | tf_op jit(solution)/shard_map/all_gather | solution.py:73
  938.5 31.0 %all_to_all.159 = bf16[128,8,512]{2,0,1:T(8,128)(2,1)S(1)} all-to-all(bf16[128,8,512]{2,0,1:T(8,128)(2,1)S(1)} %copy.81), channel_id=1, replica_groups=mesh['row'=8,'col'=4] {'row'}, dimensions={1} | all-to-all | bytes 2097152 | tf_op jit(solution)/shard_map/all_to_all | solution.py:74
  969.4 3.8 convolution_convert_fusion
  973.3 34.2 %reduce-scatter.23.cloned.1.call-done = bf16[128,1024]{1,0:T(8,128)(2,1)} async-done(((bf16[1024,1024]{1,0:T(8,128)(2,1)}), bf16[128,1024]{1,0:T(8,128)(2,1)}) %reduce-scatter.23.cloned.1.call-update) | async-done | bytes 262160 | tf_op jit(solution)/shard_map/reduce_scatter | solution.py:75
  1007.5 2.4 maximum_convert_fusion
  (126 shorter events, 49.4 us)
Async XLA Ops:
  6.5 31.9 %all-gather.12.cloned.1.call-start = ((), (), s32[]{:S(2)}) async-start(), calls=%async_computation.16 | async-start | bytes 1310720 | tf_op jit(solution)/shard_map/all_gather | solution.py:34
  8.3 101.2 %reduce-scatter.9.cloned.1.call-start = ((), (), s32[]{:S(2)}) async-start(), calls=%async_computation.17 | async-start | bytes 2359296 | tf_op jit(solution)/shard_map/reduce_scatter | solution.py:36
  75.4 0.7 copy-start.13
  75.4 1.4 copy-start.2
  75.4 2.1 copy-start
  75.4 77.4 %all-reduce.7.cloned.1.call-start = ((), (), s32[]{:S(2)}) async-start(), calls=%async_computation.18 | async-start | bytes 131072 | tf_op jit(solution)/shard_map/psum | solution.py:56
  111.6 70.6 %all-gather.14.cloned.1.call-start = ((), (), s32[]{:S(2)}) async-start(), calls=%async_computation.19 | async-start | bytes 1310720 | tf_op jit(solution)/shard_map/all_gather | solution.py:34
  155.6 98.9 %reduce-scatter.11.cloned.1.call-start = ((), (), s32[]{:S(2)}) async-start(), calls=%async_computation.20 | async-start | bytes 2359296 | tf_op jit(solution)/shard_map/reduce_scatter | solution.py:36
  220.3 0.7 copy-start.12
  220.3 77.5 %all-reduce.13.cloned.1.call-start = ((), (), s32[]{:S(2)}) async-start(), calls=%async_computation.35 | async-start | bytes 131072 | tf_op jit(solution)/shard_map/psum | solution.py:56
  256.4 69.9 %all-gather.16.cloned.1.call-start = ((), (), s32[]{:S(2)}) async-start(), calls=%async_computation.21 | async-start | bytes 1310720 | tf_op jit(solution)/shard_map/all_gather | solution.py:34
  299.7 97.9 %reduce-scatter.13.cloned.1.call-start = ((), (), s32[]{:S(2)}) async-start(), calls=%async_computation.22 | async-start | bytes 2359296 | tf_op jit(solution)/shard_map/reduce_scatter | solution.py:36
  363.4 76.7 %all-gather.18.cloned.1.call-start = ((), (), s32[]{:S(2)}) async-start(), calls=%async_computation.23 | async-start | bytes 1310720 | tf_op jit(solution)/shard_map/all_gather | solution.py:34
  417.0 94.1 %reduce-scatter.15.cloned.1.call-start = ((), (), s32[]{:S(2)}) async-start(), calls=%async_computation.24 | async-start | bytes 2359296 | tf_op jit(solution)/shard_map/reduce_scatter | solution.py:36
  477.0 61.1 %all-gather.20.cloned.1.call-start = ((), (), s32[]{:S(2)}) async-start(), calls=%async_computation.25 | async-start | bytes 1310720 | tf_op jit(solution)/shard_map/all_gather | solution.py:73
  511.2 97.2 %reduce-scatter.17.cloned.1.call-start = ((), (), s32[]{:S(2)}) async-start(), calls=%async_computation.26 | async-start | bytes 2359296 | tf_op jit(solution)/shard_map/reduce_scatter | solution.py:75
  574.2 0.7 copy-start.11
  574.2 1.4 copy-start.3
  574.2 2.1 copy-start.1
  574.2 77.4 %all-reduce.9.cloned.1.call-start = ((), (), s32[]{:S(2)}) async-start(), calls=%async_computation.27 | async-start | bytes 131072 | tf_op jit(solution)/shard_map/psum | solution.py:94
  576.4 75.3 %copy-start.7 = (bf16[128,1024]{1,0:T(8,128)(2,1)S(1)}, bf16[128,1024]{1,0:T(8,128)(2,1)}, u32[]{:S(2)}) copy-start(bf16[128,1024]{1,0:T(8,128)(2,1)} %reduce-scatter.11.cloned.1.call-done) | copy-start | bytes 786436
  576.4 75.3 %copy-start.8 = (bf16[128,1024]{1,0:T(8,128)(2,1)S(1)}, bf16[128,1024]{1,0:T(8,128)(2,1)}, u32[]{:S(2)}) copy-start(bf16[128,1024]{1,0:T(8,128)(2,1)} %reduce-scatter.13.cloned.1.call-done) | copy-start | bytes 786436
  576.4 75.3 %copy-start.9 = (bf16[128,1024]{1,0:T(8,128)(2,1)S(1)}, bf16[128,1024]{1,0:T(8,128)(2,1)}, u32[]{:S(2)}) copy-start(bf16[128,1024]{1,0:T(8,128)(2,1)} %reduce-scatter.9.cloned.1.call-done) | copy-start | bytes 786436
  610.5 70.0 %all-gather.22.cloned.1.call-start = ((), (), s32[]{:S(2)}) async-start(), calls=%async_computation.31 | async-start | bytes 1310720 | tf_op jit(solution)/shard_map/all_gather | solution.py:73
  653.8 97.6 %reduce-scatter.19.cloned.1.call-start = ((), (), s32[]{:S(2)}) async-start(), calls=%async_computation.28 | async-start | bytes 2359296 | tf_op jit(solution)/shard_map/reduce_scatter | solution.py:75
  717.2 0.7 copy-start.10
  717.2 77.3 %all-reduce.11.cloned.1.call-start = ((), (), s32[]{:S(2)}) async-start(), calls=%async_computation.34 | async-start | bytes 131072 | tf_op jit(solution)/shard_map/psum | solution.py:92
  753.4 69.8 %all-gather.24.cloned.1.call-start = ((), (), s32[]{:S(2)}) async-start(), calls=%async_computation.32 | async-start | bytes 1310720 | tf_op jit(solution)/shard_map/all_gather | solution.py:73
  796.5 97.6 %reduce-scatter.21.cloned.1.call-start = ((), (), s32[]{:S(2)}) async-start(), calls=%async_computation.29 | async-start | bytes 2359296 | tf_op jit(solution)/shard_map/reduce_scatter | solution.py:75
  859.9 76.6 %all-gather.26.cloned.1.call-start = ((), (), s32[]{:S(2)}) async-start(), calls=%async_computation.33 | async-start | bytes 1310720 | tf_op jit(solution)/shard_map/all_gather | solution.py:73
  913.5 94.0 %reduce-scatter.23.cloned.1.call-start = ((), (), s32[]{:S(2)}) async-start(), calls=%async_computation.30 | async-start | bytes 2359296 | tf_op jit(solution)/shard_map/reduce_scatter | solution.py:75
  973.2 34.2 %copy-start.4 = (bf16[128,1024]{1,0:T(8,128)(2,1)S(1)}, bf16[128,1024]{1,0:T(8,128)(2,1)}, u32[]{:S(2)}) copy-start(bf16[128,1024]{1,0:T(8,128)(2,1)} %reduce-scatter.19.cloned.1.call-done) | copy-start | bytes 786436
  973.3 34.2 %copy-start.5 = (bf16[128,1024]{1,0:T(8,128)(2,1)S(1)}, bf16[128,1024]{1,0:T(8,128)(2,1)}, u32[]{:S(2)}) copy-start(bf16[128,1024]{1,0:T(8,128)(2,1)} %reduce-scatter.21.cloned.1.call-done) | copy-start | bytes 786436
  973.3 34.2 %copy-start.6 = (bf16[128,1024]{1,0:T(8,128)(2,1)S(1)}, bf16[128,1024]{1,0:T(8,128)(2,1)}, u32[]{:S(2)}) copy-start(bf16[128,1024]{1,0:T(8,128)(2,1)} %reduce-scatter.17.cloned.1.call-done) | copy-start | bytes 786436
Sparse Core Ops, SparseCore 0:
  9.2 29.2 all-gather.11
  75.5 34.0 reduce-scatter.8
  112.4 40.3 all-reduce.6
  155.7 26.4 all-gather.13
  220.4 34.0 reduce-scatter.10
  257.2 40.5 all-reduce.12
  299.8 26.4 all-gather.15
  363.5 34.0 reduce-scatter.12
  417.2 22.8 all-gather.17
  477.1 34.0 reduce-scatter.14
  513.0 25.0 all-gather.19
  574.4 34.0 reduce-scatter.16
  611.3 40.3 all-reduce.8
  653.9 26.4 all-gather.21
  717.4 34.0 reduce-scatter.18
  754.1 40.4 all-reduce.10
  796.7 26.4 all-gather.23
  860.1 34.0 reduce-scatter.20
  913.6 22.8 all-gather.25
  973.4 34.0 reduce-scatter.22
